TPU v7x, 8 devices: a whole 2x2x1 slice. The times are simulated.
8 devices in a mesh: dp: 2 (over z, y), ep: 4 (over x, core).
Axes of the slice: x: 2, y: 2, z: 1, core: 2. Of those that a mesh axis runs over, the one named last changes fastest.
Arguments:
- x_in: bfloat16 [256, 384], P(('dp', 'ep')), parts along dimension 0
- idx_a: int32 [256, 6], P(('dp', 'ep')), parts along dimension 0
- idx_b: int32 [256, 6], P(('dp', 'ep')), parts along dimension 0
- gate_a: float32 [256, 6], P(('dp', 'ep')), parts along dimension 0
- gate_b: float32 [256, 6], P(('dp', 'ep')), parts along dimension 0
- dy_out: bfloat16 [256, 384], P(('dp', 'ep')), parts along dimension 0
- w1_a: bfloat16 [64, 384, 256], P('ep')
- w3_a: bfloat16 [64, 384, 256], P('ep')
- w2_a: bfloat16 [64, 256, 384], P('ep')
- w1_b: bfloat16 [64, 384, 256], P('ep')
- w3_b: bfloat16 [64, 384, 256], P('ep')
- w2_b: bfloat16 [64, 256, 384], P('ep')
Outputs:
- output 1: bfloat16 [256, 384], P(('dp', 'ep')), parts along dimension 0
- output 2: bfloat16 [256, 384], P(('dp', 'ep')), parts along dimension 0
- output 3: float32 [128, 384, 256], P(('dp', 'ep')), parts along dimension 0
- output 4: float32 [128, 384, 256], P(('dp', 'ep')), parts along dimension 0
- output 5: float32 [128, 256, 384], P(('dp', 'ep')), parts along dimension 0
- output 6: float32 [128, 384, 256], P(('dp', 'ep')), parts along dimension 0
- output 7: float32 [128, 384, 256], P(('dp', 'ep')), parts along dimension 0
- output 8: float32 [128, 256, 384], P(('dp', 'ep')), parts along dimension 0
- output 9: float32 [256, 6], P(('dp', 'ep')), parts along dimension 0
- output 10: float32 [256, 6], P(('dp', 'ep')), parts along dimension 0
There are 2 independent parts. A program takes and returns all parts, laid end to end along the dimension named above; an argument that names none is the same for every part.
All inputs are finite; a program needn't handle non-finite values.
Results may differ from a plain program's by a relative error of at most 0.00583839.
Values are sent between devices in bfloat16 or wider.
A program may use at most 1 GiB of HBM per device.

v0:
```python
import jax
import jax.numpy as jnp
from jax import lax
from jax.sharding import PartitionSpec as P

CAP_FACTOR = 4


def slot_maps(dev_ids, experts, capacity):
    pair_total = dev_ids.shape[0] * dev_ids.shape[1]
    flat_ids = dev_ids.reshape(-1)
    onehot = (flat_ids[:, None] == jnp.arange(experts, dtype=jnp.int32)[None, :]).astype(jnp.int32)
    pair_slot = jnp.sum(jnp.cumsum(onehot, axis=0) * onehot, axis=1) - 1
    pair_row = flat_ids * capacity + pair_slot
    pair_ids = jnp.arange(pair_total, dtype=jnp.int32)
    row_pair = jnp.full((experts * capacity,), pair_total, jnp.int32).at[pair_row].set(pair_ids)
    return pair_row, row_pair


def send_rows(rows, index, capacity):
    send_buf = jnp.take(rows, index, axis=0, mode="fill", fill_value=0)
    send_buf = send_buf.reshape((index.shape[0] // capacity, capacity) + send_buf.shape[1:])
    return lax.all_to_all(send_buf, "ep", 0, 1, tiled=True)


def send_back(rows):
    back_rows = lax.all_to_all(rows, "ep", 1, 0, tiled=True)
    return back_rows.reshape((back_rows.shape[0] * back_rows.shape[1],) + back_rows.shape[2:])


def expert_forward(u_rows, w_gate, w_up, w_down):
    pre_gate = jnp.einsum("erd,edf->erf", u_rows, w_gate, preferred_element_type=jnp.float32)
    pre_up = jnp.einsum("erd,edf->erf", u_rows, w_up, preferred_element_type=jnp.float32)
    hidden = (jax.nn.silu(pre_gate) * pre_up).astype(jnp.bfloat16)
    out_rows = jnp.einsum("erf,efd->erd", hidden, w_down, preferred_element_type=jnp.float32).astype(jnp.bfloat16)
    return pre_gate, pre_up, hidden, out_rows


def expert_backward(u_rows, dy_rows, gate_rows, w_gate, w_up, w_down):
    pre_gate, pre_up, hidden, out_rows = expert_forward(u_rows, w_gate, w_up, w_down)
    dgate_rows = jnp.einsum("erd,erd->er", dy_rows, out_rows, preferred_element_type=jnp.float32)
    d_out = (gate_rows[:, :, None] * dy_rows).astype(jnp.bfloat16)
    dw_down = jnp.einsum("erf,erd->efd", hidden, d_out, preferred_element_type=jnp.float32)
    d_hidden = jnp.einsum("erd,efd->erf", d_out, w_down, preferred_element_type=jnp.float32)
    gate_sig = jax.nn.sigmoid(pre_gate)
    d_pre_gate = (d_hidden * pre_up * gate_sig * (1.0 + pre_gate * (1.0 - gate_sig))).astype(jnp.bfloat16)
    d_pre_up = (d_hidden * jax.nn.silu(pre_gate)).astype(jnp.bfloat16)
    dw_gate = jnp.einsum("erd,erf->edf", u_rows, d_pre_gate, preferred_element_type=jnp.float32)
    dw_up = jnp.einsum("erd,erf->edf", u_rows, d_pre_up, preferred_element_type=jnp.float32)
    du_rows = (jnp.einsum("erf,edf->erd", d_pre_gate, w_gate, preferred_element_type=jnp.float32) + jnp.einsum("erf,edf->erd", d_pre_up, w_up, preferred_element_type=jnp.float32)).astype(jnp.bfloat16)
    return du_rows, dgate_rows, dw_gate, dw_up, dw_down


def combine(x_rows, gates, back_rows, pair_row):
    tok_dev, top_k = gates.shape
    out_pairs = jnp.take(back_rows, pair_row, axis=0).reshape(tok_dev, top_k, -1)
    branch = jnp.sum(gates[:, :, None] * out_pairs, axis=1)
    return (x_rows.astype(jnp.float32) + branch).astype(jnp.bfloat16)


def layer_backward(dy_rows, u_rows, gates, row_maps, capacity, w_gate, w_up, w_down):
    pair_row, row_pair = row_maps
    tok_dev, top_k = gates.shape
    dy_sent = send_rows(dy_rows, row_pair // top_k, capacity)
    gate_sent = send_rows(gates.reshape(-1), row_pair, capacity)
    u_rows, dy_sent = lax.optimization_barrier((u_rows, dy_sent))
    du_rows, dgate_rows, dw_gate, dw_up, dw_down = expert_backward(u_rows, dy_sent, gate_sent, w_gate, w_up, w_down)
    du_pairs = jnp.take(send_back(du_rows), pair_row, axis=0).reshape(tok_dev, top_k, -1)
    dx_rows = (dy_rows.astype(jnp.float32) + jnp.sum(du_pairs, axis=1, dtype=jnp.float32)).astype(jnp.bfloat16)
    dgate_out = jnp.take(send_back(dgate_rows), pair_row, axis=0).reshape(tok_dev, top_k)
    return dx_rows, dgate_out, (dw_gate, dw_up, dw_down)


def solution(mesh):
    n_group = mesh.shape["ep"]
    tok_spec = P(("dp", "ep"))
    w_spec = P("ep")

    def device_program(x_in, idx_a, idx_b, gate_a, gate_b, dy_out, w1_a, w3_a, w2_a, w1_b, w3_b, w2_b):
        tok_dev, top_k = idx_a.shape
        experts = w1_a.shape[0] * n_group
        capacity = CAP_FACTOR * tok_dev * top_k // experts
        maps_a = slot_maps(idx_a, experts, capacity)
        maps_b = slot_maps(idx_b, experts, capacity)
        u_rows_a = send_rows(x_in, maps_a[1] // top_k, capacity)
        out_a = expert_forward(u_rows_a, w1_a, w3_a, w2_a)[3]
        x_mid = combine(x_in, gate_a, send_back(out_a), maps_a[0])
        u_rows_b = send_rows(x_mid, maps_b[1] // top_k, capacity)
        out_b = expert_forward(u_rows_b, w1_b, w3_b, w2_b)[3]
        x_out = combine(x_mid, gate_b, send_back(out_b), maps_b[0])
        dx_mid, dgate_b, grads_b = layer_backward(dy_out, u_rows_b, gate_b, maps_b, capacity, w1_b, w3_b, w2_b)
        x_again, dx_mid = lax.optimization_barrier((x_in, dx_mid))
        u_again = send_rows(x_again, maps_a[1] // top_k, capacity)
        dx_in, dgate_a, grads_a = layer_backward(dx_mid, u_again, gate_a, maps_a, capacity, w1_a, w3_a, w2_a)
        return (x_out, dx_in) + grads_a + grads_b + (dgate_a, dgate_b)

    return jax.shard_map(device_program, mesh=mesh, in_specs=(tok_spec,) * 6 + (w_spec,) * 6, out_specs=(tok_spec,) * 10, check_vma=False)
```

profile of v0, /device:TPU:0, one launch (start us, length us, event | category | flops | bytes accessed | tf_op | source)
XLA Modules:
  0.0 271.2 jit_solution(11571936106024997336)
XLA Ops:
  4.9 3.3 %gather_fusion = bf16[768,384]{1,0:T(8,128)(2,1)} fusion(bf16[32,384]{1,0:T(8,128)(2,1)S(1)} %copy-done.1, s32[1024]{0:T(1024)S(1)} %pad_clamp_fusion.5), kind=kCustom, calls=%fused_computation.clone | custom fusion | bytes 1182720 | tf_op jit(solution)/shard_map/jit(_take)/gather | solution.py:21
  8.2 2.1 broadcast_select_fusion.4
  12.3 4.6 %all-to-all-start = ((bf16[64,12,384]{2,1,0:T(8,128)(2,1)}), bf16[64,12,384]{2,1,0:T(8,128)(2,1)}, u32[]{:S(2)}, u32[]{:S(2)}) async-start(bf16[64,12,384]{2,1,0:T(8,128)(2,1)} %reshape.219), calls=%async_computation | async-start | bytes 1572864 | tf_op jit(solution)/shard_map/all_to_all | solution.py:23
  20.4 5.0 %gather_fusion.4 = f32[768]{0:T(1024)S(1)} fusion(f32[192]{0:T(256)S(1)} %reshape.225, s32[1024]{0:T(1024)S(1)} %pad_clamp_fusion.1), kind=kCustom, calls=%fused_computation.2.clone | custom fusion | bytes 9216 | tf_op jit(solution)/shard_map/jit(_take)/gather | solution.py:21
  26.3 5.0 %gather_fusion.7 = f32[768]{0:T(1024)S(1)} fusion(f32[192]{0:T(256)S(1)} %reshape.228, s32[1024]{0:T(1024)S(1)} %pad_clamp_fusion), kind=kCustom, calls=%fused_computation.11.clone | custom fusion | bytes 9216 | tf_op jit(solution)/shard_map/jit(_take)/gather | solution.py:21
  34.2 3.4 %fusion.36 = f32[16,48,256]{2,1,0:T(8,128)} fusion(bf16[16,384,256]{2,1,0:T(8,128)(2,1)} %param.26, bf16[16,48,384]{2,0,1:T(8,128)(2,1)S(1)} %bitcast.124), kind=kOutput, calls=%fused_computation.72 | convolution fusion | flops 150994944 | bytes 4521984 | tf_op jit(solution)/shard_map/erd,edf->erf/dot_general | solution.py:32
  37.7 4.2 %convolution_convert_fusion.3 = bf16[16,48,384]{2,1,0:T(8,128)(2,1)} fusion(bf16[16,256,384]{2,1,0:T(8,128)(2,1)} %param.28, bf16[16,384,256]{2,1,0:T(8,128)(2,1)S(1)} %copy-done, f32[16,48,256]{2,1,0:T(8,128)} %fusion.36, bf16[16,48,384]{2,0,1:T(8,128)(2,1)} %bitcast.125), kind=kOutput, calls=%fused_computation.26 | convolution fusion | flops 303464448 | bytes 8257536 | tf_op jit(solution)/shard_map/erf,efd->erd/dot_general | solution.py:35
  43.9 4.2 %all-to-all-start.1 = ((bf16[16,48,384]{2,0,1:T(8,128)(2,1)}), bf16[16,48,384]{2,0,1:T(8,128)(2,1)}, u32[]{:S(2)}, u32[]{:S(2)}) async-start(bf16[16,48,384]{2,0,1:T(8,128)(2,1)} %copy.89), calls=%async_computation.1 | async-start | bytes 1179648 | tf_op jit(solution)/shard_map/all_to_all | solution.py:27
  48.1 3.3 %gather_fusion.5 = bf16[768,384]{1,0:T(8,128)(2,1)} fusion(bf16[32,384]{1,0:T(8,128)(2,1)S(1)} %copy-done.2, s32[1024]{0:T(1024)S(1)} %pad_clamp_fusion.3), kind=kCustom, calls=%fused_computation.5.clone | custom fusion | bytes 1182720 | tf_op jit(solution)/shard_map/jit(_take)/gather | solution.py:21
  51.5 6.5 %all-to-all-done.1 = bf16[16,48,384]{2,0,1:T(8,128)(2,1)} async-done(((bf16[16,48,384]{2,0,1:T(8,128)(2,1)}), bf16[16,48,384]{2,0,1:T(8,128)(2,1)}, u32[]{:S(2)}, u32[]{:S(2)}) %all-to-all-start.1) | async-done | bytes 589856 | tf_op jit(solution)/shard_map/all_to_all | solution.py:27
  58.0 3.2 %all-to-all-start.4 = ((f32[4,1,192]{2,1,0:T(1,128)}), f32[4,1,192]{2,1,0:T(1,128)S(1)}, u32[]{:S(2)}, u32[]{:S(2)}) async-start(f32[4,1,192]{2,1,0:T(1,128)} %reshape.415), calls=%async_computation.4 | async-start | bytes 8192 | tf_op jit(solution)/shard_map/all_to_all | solution.py:23
  61.2 2.1 copy.90
  65.3 2.8 %gather_fusion.1 = bf16[192,384]{1,0:T(8,128)(2,1)} fusion(bf16[768,384]{1,0:T(8,128)(2,1)} %reshape.220, s32[1024]{0:T(1024)S(1)} %pad_clamp_fusion.4), kind=kCustom, calls=%fused_computation.1.clone | custom fusion | bytes 295680 | tf_op jit(solution)/shard_map/jit(_take)/gather | solution.py:56
  71.1 3.3 %gather_fusion.2 = bf16[768,384]{1,0:T(8,128)(2,1)} fusion(bf16[32,384]{1,0:T(8,128)(2,1)S(1)} %add_convert_fusion.3, s32[1024]{0:T(1024)S(1)} %pad_clamp_fusion.3), kind=kCustom, calls=%fused_computation.4.clone | custom fusion | bytes 1182720 | tf_op jit(solution)/shard_map/jit(_take)/gather | solution.py:21
  74.4 3.3 %all-to-all-start.7 = ((f32[4,1,192]{2,1,0:T(1,128)}), f32[4,1,192]{2,1,0:T(1,128)S(1)}, u32[]{:S(2)}, u32[]{:S(2)}) async-start(f32[4,1,192]{2,1,0:T(1,128)} %reshape.417), calls=%async_computation.7 | async-start | bytes 8192 | tf_op jit(solution)/shard_map/all_to_all | solution.py:23
  77.6 2.5 broadcast_select_fusion
  82.1 4.2 %all-to-all-start.2 = ((bf16[64,12,384]{2,1,0:T(8,128)(2,1)}), bf16[64,12,384]{2,1,0:T(8,128)(2,1)}, u32[]{:S(2)}, u32[]{:S(2)}) async-start(bf16[64,12,384]{2,1,0:T(8,128)(2,1)} %reshape.223), calls=%async_computation.2 | async-start | bytes 1572864 | tf_op jit(solution)/shard_map/all_to_all | solution.py:23
  88.3 9.4 %all-to-all-done.2 = bf16[64,12,384]{2,1,0:T(8,128)(2,1)} async-done(((bf16[64,12,384]{2,1,0:T(8,128)(2,1)}), bf16[64,12,384]{2,1,0:T(8,128)(2,1)}, u32[]{:S(2)}, u32[]{:S(2)}) %all-to-all-start.2) | async-done | bytes 589856 | tf_op jit(solution)/shard_map/all_to_all | solution.py:23
  97.7 4.4 %all-to-all-start.5 = ((bf16[64,12,384]{2,1,0:T(8,128)(2,1)}), bf16[64,12,384]{2,1,0:T(8,128)(2,1)}, u32[]{:S(2)}, u32[]{:S(2)}) async-start(bf16[64,12,384]{2,1,0:T(8,128)(2,1)} %reshape.226), calls=%async_computation.5 | async-start | bytes 1572864 | tf_op jit(solution)/shard_map/all_to_all | solution.py:23
  106.9 6.4 %all-to-all-done.5 = bf16[64,12,384]{2,1,0:T(8,128)(2,1)} async-done(((bf16[64,12,384]{2,1,0:T(8,128)(2,1)}), bf16[64,12,384]{2,1,0:T(8,128)(2,1)}, u32[]{:S(2)}, u32[]{:S(2)}) %all-to-all-start.5) | async-done | bytes 589856 | tf_op jit(solution)/shard_map/all_to_all | solution.py:23
  114.5 3.8 %fusion.32 = f32[16,48,256]{2,1,0:T(8,128)} fusion(bf16[16,384,256]{2,1,0:T(8,128)(2,1)} %param.29, bf16[16,48,384]{2,0,1:T(8,128)(2,1)} %bitcast.110), kind=kOutput, calls=%fused_computation.69 | convolution fusion | flops 150994944 | bytes 4521984 | tf_op jit(solution)/shard_map/erd,edf->erf/dot_general | solution.py:32
  126.7 3.2 %all-to-all-start.12 = ((f32[4,1,192]{2,1,0:T(1,128)}), f32[4,1,192]{2,1,0:T(1,128)S(1)}, u32[]{:S(2)}, u32[]{:S(2)}) async-start(f32[4,1,192]{2,1,0:T(1,128)} %reshape.421), calls=%async_computation.12 | async-start | bytes 8192 | tf_op jit(solution)/shard_map/all_to_all | solution.py:27
  130.0 5.2 %convolution_convert_fusion.2 = bf16[16,48,384]{2,1,0:T(8,128)(2,1)} fusion(bf16[16,256,384]{2,1,0:T(8,128)(2,1)} %param.31, bf16[16,384,256]{2,1,0:T(8,128)(2,1)} %param.30, f32[16,48,256]{2,1,0:T(8,128)} %fusion.32, bf16[16,48,384]{2,0,1:T(8,128)(2,1)} %bitcast.111), kind=kOutput, calls=%fused_computation.25 | convolution fusion | flops 303464448 | bytes 8257536 | tf_op jit(solution)/shard_map/erf,efd->erd/dot_general | solution.py:35
  137.2 4.2 %all-to-all-start.3 = ((bf16[16,48,384]{2,0,1:T(8,128)(2,1)}), bf16[16,48,384]{2,0,1:T(8,128)(2,1)}, u32[]{:S(2)}, u32[]{:S(2)}) async-start(bf16[16,48,384]{2,0,1:T(8,128)(2,1)} %copy.100), calls=%async_computation.3 | async-start | bytes 1179648 | tf_op jit(solution)/shard_map/all_to_all | solution.py:27
  141.3 3.1 %fusion.66 = f32[16,48,384]{2,1,0:T(8,128)S(1)} fusion(bf16[16,48,256]{2,1,0:T(8,128)(2,1)} %get-tuple-element.58, bf16[16,384,256]{2,1,0:T(8,128)(2,1)} %param.29), kind=kOutput, calls=%fused_computation.164 | convolution fusion | flops 150994944 | bytes 4718592 | tf_op jit(solution)/shard_map/erf,edf->erd/dot_general | solution.py:50
  147.1 3.5 %all-to-all-done.3 = bf16[16,48,384]{2,0,1:T(8,128)(2,1)} async-done(((bf16[16,48,384]{2,0,1:T(8,128)(2,1)}), bf16[16,48,384]{2,0,1:T(8,128)(2,1)}, u32[]{:S(2)}, u32[]{:S(2)}) %all-to-all-start.3) | async-done | bytes 589856 | tf_op jit(solution)/shard_map/all_to_all | solution.py:27
  150.6 4.2 %all-to-all-start.6 = ((bf16[16,48,384]{2,0,1:T(8,128)(2,1)}), bf16[16,48,384]{2,0,1:T(8,128)(2,1)}, u32[]{:S(2)}, u32[]{:S(2)}) async-start(bf16[16,48,384]{2,0,1:T(8,128)(2,1)} %copy.109), calls=%async_computation.6 | async-start | bytes 1179648 | tf_op jit(solution)/shard_map/all_to_all | solution.py:27
  156.6 2.1 copy.101
  160.7 2.8 %gather_fusion.3 = bf16[192,384]{1,0:T(8,128)(2,1)} fusion(bf16[768,384]{1,0:T(8,128)(2,1)} %reshape.224, s32[1024]{0:T(1024)S(1)} %pad_clamp_fusion.2), kind=kCustom, calls=%fused_computation.8.clone | custom fusion | bytes 295680 | tf_op jit(solution)/shard_map/jit(_take)/gather | solution.py:56
  164.0 2.1 copy.110
  168.1 2.8 %gather_fusion.6 = bf16[192,384]{1,0:T(8,128)(2,1)} fusion(bf16[768,384]{1,0:T(8,128)(2,1)} %reshape.227, s32[1024]{0:T(1024)S(1)} %pad_clamp_fusion.2), kind=kCustom, calls=%fused_computation.9.clone | custom fusion | bytes 295680 | tf_op jit(solution)/shard_map/jit(_take)/gather | solution.py:68
  177.0 3.4 %gather_fusion.8 = bf16[768,384]{1,0:T(8,128)(2,1)} fusion(bf16[32,384]{1,0:T(8,128)(2,1)S(1)} %copy-done.1, s32[1024]{0:T(1024)} %copy-done.20), kind=kCustom, calls=%fused_computation.6.clone | custom fusion | bytes 1182720 | tf_op jit(solution)/shard_map/jit(_take)/gather | solution.py:21
  180.4 3.4 %gather_fusion.9 = bf16[768,384]{1,0:T(8,128)(2,1)} fusion(bf16[32,384]{1,0:T(8,128)(2,1)S(1)} %add_convert_fusion.1, s32[1024]{0:T(1024)} %copy-done.20), kind=kCustom, calls=%fused_computation.7.clone | custom fusion | bytes 1182720 | tf_op jit(solution)/shard_map/jit(_take)/gather | solution.py:21
  183.8 2.5 broadcast_select_fusion.2
  188.2 4.4 %all-to-all-start.8 = ((bf16[64,12,384]{2,1,0:T(8,128)(2,1)}), bf16[64,12,384]{2,1,0:T(8,128)(2,1)}, u32[]{:S(2)}, u32[]{:S(2)}) async-start(bf16[64,12,384]{2,1,0:T(8,128)(2,1)} %reshape.229), calls=%async_computation.8 | async-start | bytes 1572864 | tf_op jit(solution)/shard_map/all_to_all | solution.py:23
  192.7 5.0 %fusion.26 = f32[16,256,384]{2,1,0:T(8,128)} fusion(bf16[16,48,256]{2,1,0:T(8,128)(2,1)} %copy-done.15, bf16[16,48,384]{2,0,1:T(8,128)(2,1)} %copy-done.13), kind=kOutput, calls=%fused_computation.64 | convolution fusion | flops 150994944 | bytes 7274496 | tf_op jit(solution)/shard_map/erf,erd->efd/dot_general | solution.py:43
  197.7 3.7 %fusion.48 = f32[16,384,256]{2,1,0:T(8,128)} fusion(bf16[16,48,256]{2,1,0:T(8,128)(2,1)S(1)} %copy-done.17, bf16[16,48,384]{2,0,1:T(8,128)(2,1)S(1)} %bitcast.115), kind=kOutput, calls=%fused_computation.86 | convolution fusion | flops 150994944 | bytes 7274496 | tf_op jit(solution)/shard_map/erd,erf->edf/dot_general | solution.py:49
  203.8 4.2 %all-to-all-start.9 = ((bf16[64,12,384]{2,1,0:T(8,128)(2,1)}), bf16[64,12,384]{2,1,0:T(8,128)(2,1)}, u32[]{:S(2)}, u32[]{:S(2)}) async-start(bf16[64,12,384]{2,1,0:T(8,128)(2,1)} %reshape.230), calls=%async_computation.9 | async-start | bytes 1572864 | tf_op jit(solution)/shard_map/all_to_all | solution.py:23
  208.0 4.9 %fusion.50 = f32[16,384,256]{2,1,0:T(8,128)} fusion(bf16[16,48,256]{2,1,0:T(8,128)(2,1)} %get-tuple-element.58, bf16[16,48,384]{2,0,1:T(8,128)(2,1)} %bitcast.112), kind=kOutput, calls=%fused_computation.88 | convolution fusion | flops 150994944 | bytes 7274496 | tf_op jit(solution)/shard_map/erd,erf->edf/dot_general | solution.py:48
  216.3 2.1 copy.114
  225.3 3.7 %fusion.42 = f32[16,384,256]{2,1,0:T(8,128)} fusion(bf16[16,48,256]{2,1,0:T(8,128)(2,1)S(1)} %get-tuple-element.55, bf16[16,48,384]{2,0,1:T(8,128)(2,1)S(1)} %bitcast.119), kind=kOutput, calls=%fused_computation.80 | convolution fusion | flops 150994944 | bytes 7274496 | tf_op jit(solution)/shard_map/erd,erf->edf/dot_general | solution.py:48
  231.0 3.7 %fusion.22 = f32[16,256,384]{2,1,0:T(8,128)} fusion(bf16[16,48,256]{2,1,0:T(8,128)(2,1)S(1)} %get-tuple-element.54, bf16[16,48,384]{2,0,1:T(8,128)(2,1)S(1)} %multiply_convert_fusion), kind=kOutput, calls=%fused_computation.60 | convolution fusion | flops 150994944 | bytes 7274496 | tf_op jit(solution)/shard_map/erf,erd->efd/dot_general | solution.py:43
  236.3 3.2 %all-to-all-start.11 = ((f32[4,1,192]{2,1,0:T(1,128)}), f32[4,1,192]{2,1,0:T(1,128)S(1)}, u32[]{:S(2)}, u32[]{:S(2)}) async-start(f32[4,1,192]{2,1,0:T(1,128)} %reshape.419), calls=%async_computation.11 | async-start | bytes 8192 | tf_op jit(solution)/shard_map/all_to_all | solution.py:27
  239.6 5.0 %fusion.40 = f32[16,384,256]{2,1,0:T(8,128)} fusion(bf16[16,48,256]{2,1,0:T(8,128)(2,1)} %get-tuple-element.56, bf16[16,48,384]{2,0,1:T(8,128)(2,1)} %bitcast.116), kind=kOutput, calls=%fused_computation.78 | convolution fusion | flops 150994944 | bytes 7274496 | tf_op jit(solution)/shard_map/erd,erf->edf/dot_general | solution.py:49
  246.6 4.2 %all-to-all-start.10 = ((bf16[16,48,384]{2,0,1:T(8,128)(2,1)}), bf16[16,48,384]{2,0,1:T(8,128)(2,1)}, u32[]{:S(2)}, u32[]{:S(2)}) async-start(bf16[16,48,384]{2,0,1:T(8,128)(2,1)} %copy.119), calls=%async_computation.10 | async-start | bytes 1179648 | tf_op jit(solution)/shard_map/all_to_all | solution.py:27
  253.5 6.5 %all-to-all-done.10 = bf16[16,48,384]{2,0,1:T(8,128)(2,1)} async-done(((bf16[16,48,384]{2,0,1:T(8,128)(2,1)}), bf16[16,48,384]{2,0,1:T(8,128)(2,1)}, u32[]{:S(2)}, u32[]{:S(2)}) %all-to-all-start.10) | async-done | bytes 589856 | tf_op jit(solution)/shard_map/all_to_all | solution.py:27
  260.0 2.1 copy.120
  264.1 2.8 %gather_fusion.10 = bf16[192,384]{1,0:T(8,128)(2,1)} fusion(bf16[768,384]{1,0:T(8,128)(2,1)} %reshape.231, s32[1024]{0:T(1024)S(1)} %copy-done.23), kind=kCustom, calls=%fused_computation.10.clone | custom fusion | bytes 295680 | tf_op jit(solution)/shard_map/jit(_take)/gather | solution.py:68
  (204 shorter events, 85.0 us)
Async XLA Ops:
  0.6 37.0 %copy-start = (bf16[16,384,256]{2,1,0:T(8,128)(2,1)S(1)}, bf16[16,384,256]{2,1,0:T(8,128)(2,1)}, u32[]{:S(2)}) copy-start(bf16[16,384,256]{2,1,0:T(8,128)(2,1)} %param.27) | copy-start | bytes 9437188
  0.7 4.3 %copy-start.1 = (bf16[32,384]{1,0:T(8,128)(2,1)S(1)}, bf16[32,384]{1,0:T(8,128)(2,1)}, u32[]{:S(2)}) copy-start(bf16[32,384]{1,0:T(8,128)(2,1)} %param.20) | copy-start | bytes 73732
  4.9 5.4 %copy-start.25 = (pred[768]{0:T(1024)(128)(4,1)}, pred[768]{0:T(1024)(128)(4,1)S(1)}, u32[]{:S(2)}) copy-start(pred[768]{0:T(1024)(128)(4,1)S(1)} %get-tuple-element.52) | copy-start | bytes 2308
  4.9 5.4 %copy-start.20 = (s32[1024]{0:T(1024)}, s32[1024]{0:T(1024)S(1)}, u32[]{:S(2)}) copy-start(s32[1024]{0:T(1024)S(1)} %pad_clamp_fusion.5) | copy-start | bytes 12292
  8.2 8.7 %copy-start.21 = (s32[32,6]{0,1:T(8,128)S(1)}, s32[32,6]{0,1:T(8,128)}, u32[]{:S(2)}) copy-start(s32[32,6]{0,1:T(8,128)} %param.22) | copy-start | bytes 2308
  8.2 8.8 %copy-start.29 = (f32[32,6]{0,1:T(8,128)S(1)}, f32[32,6]{0,1:T(8,128)}, u32[]{:S(2)}) copy-start(f32[32,6]{0,1:T(8,128)} %param.23) | copy-start | bytes 2308
  8.2 12.0 %copy-start.30 = (f32[32,6]{0,1:T(8,128)S(1)}, f32[32,6]{0,1:T(8,128)}, u32[]{:S(2)}) copy-start(f32[32,6]{0,1:T(8,128)} %param.24) | copy-start | bytes 2308
  12.3 19.9 %all-to-all-start = ((bf16[64,12,384]{2,1,0:T(8,128)(2,1)}), bf16[64,12,384]{2,1,0:T(8,128)(2,1)}, u32[]{:S(2)}, u32[]{:S(2)}) async-start(bf16[64,12,384]{2,1,0:T(8,128)(2,1)} %reshape.219), calls=%async_computation | async-start | bytes 1572864 | tf_op jit(solution)/shard_map/all_to_all | solution.py:23
  33.4 0.8 copy-start.14
  41.9 6.2 %copy-start.2 = (bf16[32,384]{1,0:T(8,128)(2,1)S(1)}, bf16[32,384]{1,0:T(8,128)(2,1)}, u32[]{:S(2)}) copy-start(bf16[32,384]{1,0:T(8,128)(2,1)} %param.25) | copy-start | bytes 73732
  43.9 14.0 %all-to-all-start.1 = ((bf16[16,48,384]{2,0,1:T(8,128)(2,1)}), bf16[16,48,384]{2,0,1:T(8,128)(2,1)}, u32[]{:S(2)}, u32[]{:S(2)}) async-start(bf16[16,48,384]{2,0,1:T(8,128)(2,1)} %copy.89), calls=%async_computation.1 | async-start | bytes 1179648 | tf_op jit(solution)/shard_map/all_to_all | solution.py:27
  51.4 18.5 %copy-start.27 = (pred[192]{0:T(512)(128)(4,1)}, pred[192]{0:T(512)(128)(4,1)S(1)}, u32[]{:S(2)}) copy-start(pred[192]{0:T(512)(128)(4,1)S(1)} %get-tuple-element.50) | copy-start | bytes 580
  51.4 18.5 %copy-start.22 = (s32[1024]{0:T(1024)}, s32[1024]{0:T(1024)S(1)}, u32[]{:S(2)}) copy-start(s32[1024]{0:T(1024)S(1)} %pad_clamp_fusion.4) | copy-start | bytes 12292
  58.0 16.4 %all-to-all-start.4 = ((f32[4,1,192]{2,1,0:T(1,128)}), f32[4,1,192]{2,1,0:T(1,128)S(1)}, u32[]{:S(2)}, u32[]{:S(2)}) async-start(f32[4,1,192]{2,1,0:T(1,128)} %reshape.415), calls=%async_computation.4 | async-start | bytes 8192 | tf_op jit(solution)/shard_map/all_to_all | solution.py:23
  74.4 7.8 %all-to-all-start.7 = ((f32[4,1,192]{2,1,0:T(1,128)}), f32[4,1,192]{2,1,0:T(1,128)S(1)}, u32[]{:S(2)}, u32[]{:S(2)}) async-start(f32[4,1,192]{2,1,0:T(1,128)} %reshape.417), calls=%async_computation.7 | async-start | bytes 8192 | tf_op jit(solution)/shard_map/all_to_all | solution.py:23
  80.1 22.0 %copy-start.24 = (s32[192]{0:T(256)S(1)}, s32[192]{0:T(256)}, u32[]{:S(2)}) copy-start(s32[192]{0:T(256)} %get-tuple-element.64) | copy-start | bytes 2308
  82.1 15.6 %all-to-all-start.2 = ((bf16[64,12,384]{2,1,0:T(8,128)(2,1)}), bf16[64,12,384]{2,1,0:T(8,128)(2,1)}, u32[]{:S(2)}, u32[]{:S(2)}) async-start(bf16[64,12,384]{2,1,0:T(8,128)(2,1)} %reshape.223), calls=%async_computation.2 | async-start | bytes 1572864 | tf_op jit(solution)/shard_map/all_to_all | solution.py:23
  97.7 15.6 %all-to-all-start.5 = ((bf16[64,12,384]{2,1,0:T(8,128)(2,1)}), bf16[64,12,384]{2,1,0:T(8,128)(2,1)}, u32[]{:S(2)}, u32[]{:S(2)}) async-start(bf16[64,12,384]{2,1,0:T(8,128)(2,1)} %reshape.226), calls=%async_computation.5 | async-start | bytes 1572864 | tf_op jit(solution)/shard_map/all_to_all | solution.py:23
  114.5 4.1 %copy-start.3 = (bf16[16,384,256]{2,1,0:T(8,128)(2,1)S(1)}, bf16[16,384,256]{2,1,0:T(8,128)(2,1)}, u32[]{:S(2)}) copy-start(bf16[16,384,256]{2,1,0:T(8,128)(2,1)} %param.29) | copy-start | bytes 9437188
  114.5 4.1 %copy-start.5 = (bf16[16,4,12,384]{3,0,2,1:T(8,128)(2,1)S(1)}, bf16[16,4,12,384]{3,0,2,1:T(8,128)(2,1)}, u32[]{:S(2)}) copy-start(bf16[16,4,12,384]{3,0,2,1:T(8,128)(2,1)} %copy.97) | copy-start | bytes 1769476
  118.4 2.1 copy-start.8
  118.6 2.6 copy-start.13
  120.5 1.9 copy-start.12
  124.5 0.7 copy-start.15
  126.7 10.4 %all-to-all-start.12 = ((f32[4,1,192]{2,1,0:T(1,128)}), f32[4,1,192]{2,1,0:T(1,128)S(1)}, u32[]{:S(2)}, u32[]{:S(2)}) async-start(f32[4,1,192]{2,1,0:T(1,128)} %reshape.421), calls=%async_computation.12 | async-start | bytes 8192 | tf_op jit(solution)/shard_map/all_to_all | solution.py:27
  137.2 13.4 %all-to-all-start.3 = ((bf16[16,48,384]{2,0,1:T(8,128)(2,1)}), bf16[16,48,384]{2,0,1:T(8,128)(2,1)}, u32[]{:S(2)}, u32[]{:S(2)}) async-start(bf16[16,48,384]{2,0,1:T(8,128)(2,1)} %copy.100), calls=%async_computation.3 | async-start | bytes 1179648 | tf_op jit(solution)/shard_map/all_to_all | solution.py:27
  141.3 3.2 %copy-start.9 = (bf16[16,384,256]{2,1,0:T(8,128)(2,1)S(1)}, bf16[16,384,256]{2,1,0:T(8,128)(2,1)}, u32[]{:S(2)}) copy-start(bf16[16,384,256]{2,1,0:T(8,128)(2,1)} %param.30) | copy-start | bytes 9437188
  141.3 3.2 %copy-start.16 = (bf16[16,48,256]{2,1,0:T(8,128)(2,1)S(1)}, bf16[16,48,256]{2,1,0:T(8,128)(2,1)}, u32[]{:S(2)}) copy-start(bf16[16,48,256]{2,1,0:T(8,128)(2,1)} %get-tuple-element.57) | copy-start | bytes 1179652
  150.6 13.4 %all-to-all-start.6 = ((bf16[16,48,384]{2,0,1:T(8,128)(2,1)}), bf16[16,48,384]{2,0,1:T(8,128)(2,1)}, u32[]{:S(2)}, u32[]{:S(2)}) async-start(bf16[16,48,384]{2,0,1:T(8,128)(2,1)} %copy.109), calls=%async_computation.6 | async-start | bytes 1179648 | tf_op jit(solution)/shard_map/all_to_all | solution.py:27
  180.4 3.4 %copy-start.26 = (pred[768]{0:T(1024)(128)(4,1)S(1)}, pred[768]{0:T(1024)(128)(4,1)}, u32[]{:S(2)}) copy-start(pred[768]{0:T(1024)(128)(4,1)} %copy-done.25) | copy-start | bytes 2308
  188.2 15.6 %all-to-all-start.8 = ((bf16[64,12,384]{2,1,0:T(8,128)(2,1)}), bf16[64,12,384]{2,1,0:T(8,128)(2,1)}, u32[]{:S(2)}, u32[]{:S(2)}) async-start(bf16[64,12,384]{2,1,0:T(8,128)(2,1)} %reshape.229), calls=%async_computation.8 | async-start | bytes 1572864 | tf_op jit(solution)/shard_map/all_to_all | solution.py:23
  192.6 5.0 %copy-start.6 = (bf16[16,4,12,384]{3,0,2,1:T(8,128)(2,1)S(1)}, bf16[16,4,12,384]{3,0,2,1:T(8,128)(2,1)}, u32[]{:S(2)}) copy-start(bf16[16,4,12,384]{3,0,2,1:T(8,128)(2,1)} %copy.97) | copy-start | bytes 1769476
  192.7 5.0 %copy-start.17 = (bf16[16,48,256]{2,1,0:T(8,128)(2,1)S(1)}, bf16[16,48,256]{2,1,0:T(8,128)(2,1)}, u32[]{:S(2)}) copy-start(bf16[16,48,256]{2,1,0:T(8,128)(2,1)} %get-tuple-element.57) | copy-start | bytes 1179652
  203.8 15.6 %all-to-all-start.9 = ((bf16[64,12,384]{2,1,0:T(8,128)(2,1)}), bf16[64,12,384]{2,1,0:T(8,128)(2,1)}, u32[]{:S(2)}, u32[]{:S(2)}) async-start(bf16[64,12,384]{2,1,0:T(8,128)(2,1)} %reshape.230), calls=%async_computation.9 | async-start | bytes 1572864 | tf_op jit(solution)/shard_map/all_to_all | solution.py:23
  208.0 4.9 %copy-start.31 = (f32[192]{0:T(256)S(1)}, f32[192]{0:T(256)}, u32[]{:S(2)}) copy-start(f32[192]{0:T(256)} %get-tuple-element.46) | copy-start | bytes 2308
  212.9 7.9 %copy-start.19 = (f32[16,48]{0,1:T(8,128)S(1)}, f32[16,48]{0,1:T(8,128)}, u32[]{:S(2)}) copy-start(f32[16,48]{0,1:T(8,128)} %reshape.408) | copy-start | bytes 9220
  219.4 2.1 copy-start.7
  220.9 2.0 copy-start.4
  220.9 2.1 copy-start.10
  236.3 10.3 %all-to-all-start.11 = ((f32[4,1,192]{2,1,0:T(1,128)}), f32[4,1,192]{2,1,0:T(1,128)S(1)}, u32[]{:S(2)}, u32[]{:S(2)}) async-start(f32[4,1,192]{2,1,0:T(1,128)} %reshape.419), calls=%async_computation.11 | async-start | bytes 8192 | tf_op jit(solution)/shard_map/all_to_all | solution.py:27
  239.5 5.0 %copy-start.11 = (f32[16,48,384]{2,1,0:T(8,128)S(1)}, f32[16,48,384]{2,1,0:T(8,128)}, u32[]{:S(2)}) copy-start(f32[16,48,384]{2,1,0:T(8,128)} %fusion.67) | copy-start | bytes 3538948
  239.6 5.0 %copy-start.18 = (bf16[16,48,256]{2,1,0:T(8,128)(2,1)S(1)}, bf16[16,48,256]{2,1,0:T(8,128)(2,1)}, u32[]{:S(2)}) copy-start(bf16[16,48,256]{2,1,0:T(8,128)(2,1)} %get-tuple-element.56) | copy-start | bytes 1179652
  244.6 6.9 %copy-start.23 = (s32[1024]{0:T(1024)S(1)}, s32[1024]{0:T(1024)}, u32[]{:S(2)}) copy-start(s32[1024]{0:T(1024)} %copy-done.22) | copy-start | bytes 12292
  244.6 8.1 %copy-start.28 = (pred[192]{0:T(512)(128)(4,1)S(1)}, pred[192]{0:T(512)(128)(4,1)}, u32[]{:S(2)}) copy-start(pred[192]{0:T(512)(128)(4,1)} %copy-done.27) | copy-start | bytes 580
  246.6 13.4 %all-to-all-start.10 = ((bf16[16,48,384]{2,0,1:T(8,128)(2,1)}), bf16[16,48,384]{2,0,1:T(8,128)(2,1)}, u32[]{:S(2)}, u32[]{:S(2)}) async-start(bf16[16,48,384]{2,0,1:T(8,128)(2,1)} %copy.119), calls=%async_computation.10 | async-start | bytes 1179648 | tf_op jit(solution)/shard_map/all_to_all | solution.py:27
where the time goes:
time: 274 us; the launch traced here: 271 us
  local copies, waits for them, and re-layouts  101 us (37%)
  matrix products  58.1 us (21%)
  starting transfers between devices  51.4 us (19%)
  waiting for transfers between devices  34.2 us (12%)
  other arithmetic  25.4 us (9%)
    all_to_all x7, starting transfers between devices, send_rows(): return lax.all_to_all(send_buf, 'ep', 0, 1, tiled=True)  28.3 us
    gather x7, local copies, waits for them, and re-layouts, send_rows(): send_buf = jnp.take(rows, index, axis=0, mode='fill', fill_value=0)  26.5 us
    all_to_all x6, starting transfers between devices, send_back(): back_rows = lax.all_to_all(rows, 'ep', 1, 0, tiled=True)  23.2 us
    all_to_all x7, waiting for transfers between devices, send_rows(): return lax.all_to_all(send_buf, 'ep', 0, 1, tiled=True)  17.2 us
    all_to_all x6, waiting for transfers between devices, send_back(): back_rows = lax.all_to_all(rows, 'ep', 1, 0, tiled=True)  17 us
    dot_general x4, matrix products, expert_forward(): jnp.einsum('erf,efd->erd', hidden, w_down, preferred_element_type=jnp.flo...  10.9 us
    unnamed x78, local copies, waits for them, and re-layouts  10.6 us
    reshape x5, local copies, waits for them, and re-layouts, send_rows(): send_buf.reshape((index.shape[0] // capacity, capacity) + send_buf.shape[...  10 us
  transfers between devices with their start and end apart: 13, of which 8 were waited for; matrix products, arithmetic and copies ran while one was open for 35% of the time, Pallas kernels for 0%

commit v1 on v0

v1 whole, which is shorter than its diff:
```python
import functools

import jax
import jax.numpy as jnp
from jax import lax
from jax.experimental import pallas as pl
from jax.experimental.pallas import tpu as pltpu
from jax.sharding import PartitionSpec as P

MESH = pl.DeviceIdType.MESH
F32 = jnp.float32
BF16 = jnp.bfloat16
NN = (((1,), (0,)), ((), ()))
NT = (((1,), (1,)), ((), ()))
TN = (((0,), (0,)), ((), ()))
LANES = 128
PAD = 8


def mm(lhs, rhs, dims=NN):
    return lax.dot_general(lhs, rhs, dims, preferred_element_type=F32)


def step_kernel(
    n, x_ref, dy_ref, idx_a_ref, idx_b_ref, gate_a_ref, gate_b_ref,
    w1_a, w3_a, w2_a, w1_b, w3_b, w2_b,
    x_out_ref, dx_in_ref, dgate_a_ref, dgate_b_ref, xg_a, xg_b, dyg_a, dyg_b, ids_ref, gates_ref, h_out, da_out, db_out,
    w1_v, w3_v, w2_v, h_v, da_v, db_v, planes, meta, meta_own, acc, acc_fwd, recv, own, dg, dg_send, dg_recv, xg_first,
    w_sem, f_sem, send_sem, recv_sem,
):
    local_experts = w1_a.shape[0]
    tok = x_ref.shape[0]
    width = x_ref.shape[1]
    top = idx_a_ref.shape[1]
    rows = n * tok
    me = lax.axis_index("ep")
    first_expert = me * local_experts
    weights = ((w1_a, w3_a, w2_a), (w1_b, w3_b, w2_b))
    slots = (w1_v, w3_v, w2_v)

    def weight_copy(layer, kind, e):
        return pltpu.make_async_copy(weights[layer][kind].at[e], slots[kind].at[layer, e], w_sem.at[layer, kind, e])

    for layer in range(2):
        for kind in range(3):
            @pl.loop(0, local_experts)
            def _(e):
                weight_copy(layer, kind, e).start()

    barrier = pltpu.get_barrier_semaphore()
    for k in range(1, n):
        pl.semaphore_signal(barrier, inc=1, device_id={"ep": lax.rem(me + k, n)}, device_id_type=MESH)
    pl.semaphore_wait(barrier, n - 1)

    def exchange(event, source, target):
        copies = []
        for k in (2, 1, 3):
            peer = lax.rem(me + k, n)
            copy = pltpu.make_async_remote_copy(
                src_ref=source(peer), dst_ref=target.at[me], send_sem=send_sem.at[event, k - 1], recv_sem=recv_sem.at[event, k - 1],
                device_id={"ep": peer}, device_id_type=MESH)
            copy.start()
            copies.append(copy)
        return copies

    def wait(copies):
        for copy in copies:
            copy.wait()

    first_x = exchange(0, lambda peer: x_ref, xg_first)
    xg_first[me] = x_ref[...]

    planes[...] = jnp.full_like(planes, -1.0)
    planes[0, :, 0:top] = idx_a_ref[...].astype(F32)
    planes[1, :, 0:top] = idx_b_ref[...].astype(F32)
    planes[2, :, 0:top] = gate_a_ref[...]
    planes[3, :, 0:top] = gate_b_ref[...]
    lane = lax.broadcasted_iota(jnp.int32, (tok, LANES), 1)
    packed = planes[0]
    for p in range(1, 4):
        packed = jnp.where(lane < p * PAD, packed, pltpu.roll(planes[p], p * PAD, 1))
    meta_own[...] = packed
    meta[me] = packed
    sent_meta = exchange(1, lambda peer: meta_own, meta)
    sent_dy = exchange(2, lambda peer: dy_ref, dyg_b)
    dyg_b[me] = dy_ref[...]

    def flat(ref):
        value = ref[...]
        return value.reshape(value.shape[0] * value.shape[1], value.shape[2])

    def pair_gate(layer, e):
        hit = ids_ref[layer] == (first_expert + e).astype(F32)
        gate = jnp.sum(jnp.where(hit, gates_ref[layer], 0.0), axis=1, keepdims=True)
        return hit, gate

    def hidden_of(layer, e, u_rows):
        pre_gate = mm(u_rows, w1_v[layer, e])
        pre_up = mm(u_rows, w3_v[layer, e])
        sig = jax.nn.sigmoid(pre_gate)
        silu = pre_gate * sig
        return pre_gate, pre_up, sig, silu, (silu * pre_up).astype(BF16)

    def add_rows(total, value):
        total[...] += value.reshape(total.shape)

    def forward(layer, u_ref, total, wait_weights):
        total[...] = jnp.zeros_like(total)
        u_rows = flat(u_ref)

        @pl.loop(0, local_experts)
        def _(e):
            if wait_weights:
                weight_copy(layer, 0, e).wait()
                weight_copy(layer, 1, e).wait()
            h_v[layer, e] = hidden_of(layer, e, u_rows)[4]

        if wait_weights:
            wait(sent_meta)
            all_meta = flat(meta)
            wide_lane = lax.broadcasted_iota(jnp.int32, (rows, LANES), 1)
            for which in range(2):
                ids = pltpu.roll(all_meta, LANES - which * PAD, 1) if which else all_meta
                ids_ref[which] = jnp.where(wide_lane < top, ids, -1.0)
                gates_ref[which] = pltpu.roll(all_meta, LANES - (2 + which) * PAD, 1)

        @pl.loop(0, local_experts)
        def _(e):
            if wait_weights:
                weight_copy(layer, 2, e).wait()
            gate = pair_gate(layer, e)[1]
            out_rows = mm(h_v[layer, e], w2_v[layer, e]).astype(BF16).astype(F32)
            add_rows(total, jnp.where(gate > 0.0, gate * out_rows, 0.0))

    def factor_copies(layer, e):
        return [pltpu.make_async_copy(v.at[layer, e], o.at[layer, e], f_sem.at[layer, i, e])
                for i, (v, o) in enumerate(((h_v, h_out), (da_v, da_out), (db_v, db_out)))]

    def backward(layer, u_ref, dy_all_ref, total):
        total[...] = jnp.zeros_like(total)
        dg[layer] = jnp.zeros_like(dg[layer])
        u_rows = flat(u_ref)
        dy_rows = flat(dy_all_ref)

        @pl.loop(0, local_experts)
        def _(e):
            pre_gate, pre_up, sig, silu, hidden = hidden_of(layer, e, u_rows)
            hit, gate = pair_gate(layer, e)
            live = gate > 0.0
            wide = dy_rows.astype(F32)
            q = (gate * wide).astype(BF16)
            d_hidden = mm(q, w2_v[layer, e], NT)
            d_gate = jnp.where(live, d_hidden * pre_up * sig * (1.0 + pre_gate * (1.0 - sig)), 0.0).astype(BF16)
            d_up = jnp.where(live, d_hidden * silu, 0.0).astype(BF16)
            du = mm(d_gate, w1_v[layer, e], NT) + mm(d_up, w3_v[layer, e], NT)
            add_rows(total, du.astype(BF16).astype(F32))
            out_rows = mm(hidden, w2_v[layer, e]).astype(BF16).astype(F32)
            dgate_col = jnp.sum(wide * out_rows, axis=1, keepdims=True)
            dg[layer] += jnp.where(hit, dgate_col, 0.0)
            h_v[layer, e] = jnp.where(live, hidden.astype(F32), 0.0).astype(BF16)
            da_v[layer, e] = d_gate
            db_v[layer, e] = d_up
            for copy in factor_copies(layer, e):
                copy.start()

    def finish_factors(layer):
        @pl.loop(0, local_experts)
        def _(e):
            for copy in factor_copies(layer, e):
                copy.wait()

    def reduced(event, base, total):
        value = base.astype(F32) + total[me]
        for k in range(1, n):
            value += recv[event, lax.rem(me + k, n)]
        return value.astype(BF16)

    wait(first_x)
    forward(0, xg_first, acc, True)
    sent = exchange(3, lambda peer: acc.at[peer], recv.at[0])
    wait(sent)
    x_mid = reduced(0, x_ref[...], acc)
    own[0] = x_mid
    xg_b[me] = x_mid
    sent_mid = exchange(4, lambda peer: own.at[0], xg_b)

    @pl.loop(0, local_experts)
    def _(e):
        for kind in range(3):
            weight_copy(1, kind, e).wait()

    wait(sent_dy)
    wait(sent_mid)
    again = exchange(5, lambda peer: x_ref, xg_a)
    xg_a[me] = x_ref[...]

    backward(1, xg_b, dyg_b, acc)
    sent = exchange(6, lambda peer: acc.at[peer], recv.at[1])
    finish_factors(1)
    h_keep = None
    del h_keep
    forward(1, xg_b, acc_fwd, False)
    sent_out = exchange(7, lambda peer: acc_fwd.at[peer], recv.at[2])
    wait(sent)
    dx_mid = reduced(1, dy_ref[...], acc)
    own[1] = dx_mid
    dyg_a[me] = dx_mid
    sent_mid = exchange(8, lambda peer: own.at[1], dyg_a)
    wait(sent_out)
    x_out_ref[...] = reduced(2, own[0], acc_fwd)
    wait(again)
    wait(sent_mid)

    backward(0, xg_a, dyg_a, acc)
    sent = exchange(9, lambda peer: acc.at[peer], recv.at[3])
    both = jnp.where(lax.broadcasted_iota(jnp.int32, (rows, LANES), 1) < PAD, dg[0], pltpu.roll(dg[1], PAD, 1))
    dg_send[...] = both.reshape(dg_send.shape)
    sent_dg = exchange(10, lambda peer: dg_send.at[peer], dg_recv)
    finish_factors(0)
    wait(sent)
    dx_in_ref[...] = reduced(3, dy_ref[...] if False else own[1], acc)
    wait(sent_dg)
    value = dg_send[me]
    for k in range(1, n):
        value += dg_recv[lax.rem(me + k, n)]
    dgate_a_ref[...] = value[:, 0:top]
    dgate_b_ref[...] = pltpu.roll(value, LANES - PAD, 1)[:, 0:top]


def grads_kernel(
    xa, xb, dya, dyb, ids_ref, gates_ref, h_ref, da_ref, db_ref, x_out_in, dx_in_in, dga_in, dgb_in,
    dw1_a, dw3_a, dw2_a, dw1_b, dw3_b, dw2_b, x_out, dx_in, dga, dgb,
):
    e = pl.program_id(0)
    expert = lax.axis_index("ep") * pl.num_programs(0) + e

    @pl.when(e == 0)
    def _():
        x_out[...] = x_out_in[...]
        dx_in[...] = dx_in_in[...]
        dga[...] = dga_in[...]
        dgb[...] = dgb_in[...]

    for layer, (x, dy, dw1, dw3, dw2) in enumerate(((xa, dya, dw1_a, dw3_a, dw2_a), (xb, dyb, dw1_b, dw3_b, dw2_b))):
        gate = jnp.sum(jnp.where(ids_ref[layer] == expert.astype(F32), gates_ref[layer], 0.0), axis=1, keepdims=True)
        q = (gate * dy[...].astype(F32)).astype(BF16)
        dw2[0] = mm(h_ref[layer, 0], q, TN)
        dw1[0] = mm(x[...], da_ref[layer, 0], TN)
        dw3[0] = mm(x[...], db_ref[layer, 0], TN)


def solution(mesh):
    n = mesh.shape["ep"]
    tok_spec = P(("dp", "ep"))
    w_spec = P("ep")

    def device_program(x_in, idx_a, idx_b, gate_a, gate_b, dy_out, w1_a, w3_a, w2_a, w1_b, w3_b, w2_b):
        tok, width = x_in.shape
        top = idx_a.shape[1]
        experts, _, ff = w1_a.shape
        rows = n * tok
        vmem = pl.BlockSpec(memory_space=pltpu.VMEM)
        anyw = pl.BlockSpec(memory_space=pl.ANY)
        sds = jax.ShapeDtypeStruct
        factor = sds((2, experts, rows, ff), BF16)
        gathered = sds((n, tok, width), BF16)
        outs = pl.pallas_call(
            functools.partial(step_kernel, n),
            out_shape=(
                sds((tok, width), BF16), sds((tok, width), BF16), sds((tok, top), F32), sds((tok, top), F32),
                gathered, gathered, gathered, gathered,
                sds((2, rows, LANES), F32), sds((2, rows, LANES), F32), factor, factor, factor),
            in_specs=[vmem] * 6 + [anyw] * 6,
            out_specs=(vmem,) * 10 + (anyw,) * 3,
            scratch_shapes=[
                pltpu.VMEM((2, experts, width, ff), BF16), pltpu.VMEM((2, experts, width, ff), BF16), pltpu.VMEM((2, experts, ff, width), BF16),
                pltpu.VMEM((2, experts, rows, ff), BF16), pltpu.VMEM((2, experts, rows, ff), BF16), pltpu.VMEM((2, experts, rows, ff), BF16),
                pltpu.VMEM((4, tok, LANES), F32), pltpu.VMEM((n, tok, LANES), F32), pltpu.VMEM((tok, LANES), F32),
                pltpu.VMEM((n, tok, width), F32), pltpu.VMEM((n, tok, width), F32), pltpu.VMEM((4, n, tok, width), F32), pltpu.VMEM((2, tok, width), BF16),
                pltpu.VMEM((2, rows, LANES), F32), pltpu.VMEM((n, tok, LANES), F32), pltpu.VMEM((n, tok, LANES), F32),
                pltpu.VMEM((n, tok, width), BF16),
                pltpu.SemaphoreType.DMA((2, 3, experts)), pltpu.SemaphoreType.DMA((2, 3, experts)),
                pltpu.SemaphoreType.DMA((11, n - 1)), pltpu.SemaphoreType.DMA((11, n - 1)),
            ],
            compiler_params=pltpu.CompilerParams(collective_id=0, has_side_effects=True, vmem_limit_bytes=56 << 20),
            name="moe_step",
        )(x_in, dy_out, idx_a, idx_b, gate_a, gate_b, w1_a, w3_a, w2_a, w1_b, w3_b, w2_b)
        x_out, dx_in, dga, dgb, xa, xb, dya, dyb, ids, gates, h, da, db = outs
        flat = lambda v: v.reshape(rows, width)
        whole = lambda v: pl.BlockSpec(v.shape, lambda e: (0,) * v.ndim)
        fac = pl.BlockSpec((2, 1, rows, ff), lambda e: (0, e, 0, 0))
        dw_up = pl.BlockSpec((1, width, ff), lambda e: (e, 0, 0))
        dw_down = pl.BlockSpec((1, ff, width), lambda e: (e, 0, 0))
        small = [flat(xa), flat(xb), flat(dya), flat(dyb), ids, gates]
        last = [x_out, dx_in, dga, dgb]
        up, down = sds((experts, width, ff), F32), sds((experts, ff, width), F32)
        res = pl.pallas_call(
            grads_kernel,
            grid=(experts,),
            out_shape=(up, up, down, up, up, down) + tuple(sds(v.shape, v.dtype) for v in last),
            in_specs=[whole(v) for v in small] + [fac] * 3 + [whole(v) for v in last],
            out_specs=(dw_up, dw_up, dw_down, dw_up, dw_up, dw_down) + tuple(whole(v) for v in last),
            compiler_params=pltpu.CompilerParams(dimension_semantics=("arbitrary",), vmem_limit_bytes=32 << 20),
            name="moe_grads",
        )(*small, h, da, db, *last)
        g = res[:6]
        x_out, dx_in, dga, dgb = res[6:]
        return (x_out, dx_in) + g + (dga, dgb)

    return jax.shard_map(device_program, mesh=mesh, in_specs=(tok_spec,) * 6 + (w_spec,) * 6, out_specs=(tok_spec,) * 10, check_vma=False)
```

time: 274 us -> 97.7 us (0.36)
  local copies, waits for them, and re-layouts: 101 us -> 19.9 us
  Pallas kernels: 0 us -> 76.4 us
  matrix products: 58.1 us -> 0 us
  starting transfers between devices: 51.4 us -> 0 us
  waiting for transfers between devices: 34.2 us -> 0 us
  other arithmetic: 25.4 us -> 0 us
    pallas_call x0 -> x2, Pallas kernels: none -> 76.4 us  [the longest x1 61.2 us: device_program(): pl.pallas_call(functools.partial(step_kernel, n), out_shape=(sds((tok, wi...]
    dot_general x22 -> x0, matrix products: 58.1 us -> none  [the longest x4 10.9 us: expert_forward(): jnp.einsum('erf,efd->erd', hidden, w_down, preferred_element_type=jnp.flo...]
    all_to_all x13 -> x0, starting transfers between devices: 51.4 us -> none  [the longest x7 28.3 us: send_rows(): return lax.all_to_all(send_buf, 'ep', 0, 1, tiled=True)]
    gather x13 -> x0, local copies, waits for them, and re-layouts: 40 us -> none  [the longest x7 26.5 us: send_rows(): send_buf = jnp.take(rows, index, axis=0, mode='fill', fill_value=0)]
    all_to_all x13 -> x0, waiting for transfers between devices: 34.2 us -> none  [the longest x7 17.2 us: send_rows(): return lax.all_to_all(send_buf, 'ep', 0, 1, tiled=True)]
    reshape x15 -> x0, local copies, waits for them, and re-layouts: 18.6 us -> none  [the longest x5 10 us: send_rows(): send_buf.reshape((index.shape[0] // capacity, capacity) + send_buf.shape[...]
    all_to_all x18 -> x0, local copies, waits for them, and re-layouts: 17.3 us -> none  [the longest x8 8.76 us: send_rows(): return lax.all_to_all(send_buf, 'ep', 0, 1, tiled=True)]
    convert_element_type x8 -> x0, local copies, waits for them, and re-layouts: 9.95 us -> none  [the longest x2 4 us: expert_forward(): jnp.einsum('erf,efd->erd', hidden, w_down, preferred_element_type=jnp.flo...]
  transfers between devices with their start and end apart: 13 -> 0, of which waited for: 8 -> 0; matrix products, arithmetic and copies ran while one was open for 35% -> 0% of each run, Pallas kernels for 0% -> 0%
where the time goes in v1:
time: 97.7 us; the launch traced here: 96.9 us
  Pallas kernels  76.4 us (78%)
  local copies, waits for them, and re-layouts  19.9 us (20%)
    pallas_call x1, Pallas kernels, device_program(): pl.pallas_call(functools.partial(step_kernel, n), out_shape=(sds((tok, wi...  61.2 us
    unnamed x32, local copies, waits for them, and re-layouts  19.9 us
    pallas_call x1, Pallas kernels, device_program(): pl.pallas_call(grads_kernel, grid=(experts,), out_shape=(up, up, down, up...  15.1 us

profile of v1, /device:TPU:0, one launch (start us, length us, event | category | flops | bytes accessed | tf_op | source)
XLA Modules:
  0.0 96.9 jit_solution(2380495525902011106)
XLA Ops:
  0.6 1.4 %copy.22.idx_a_ref = s32[32,6]{1,0:T(8,128)} copy(s32[32,6]{0,1:T(8,128)} %param.13) | data formatting | bytes 1536 | tf_op args[1]
  2.0 1.4 %copy.23.idx_b_ref = s32[32,6]{1,0:T(8,128)} copy(s32[32,6]{0,1:T(8,128)} %param.14) | data formatting | bytes 1536 | tf_op args[2]
  3.4 1.4 %copy.24.gate_a_ref = f32[32,6]{1,0:T(8,128)} copy(f32[32,6]{0,1:T(8,128)} %param.15) | data formatting | bytes 1536 | tf_op args[3]
  4.8 1.4 %copy.25.gate_b_ref = f32[32,6]{1,0:T(8,128)} copy(f32[32,6]{0,1:T(8,128)} %param.16) | data formatting | bytes 1536 | tf_op args[4]
  6.1 61.2 %moe_step.1 = (bf16[32,384]{1,0:T(8,128)(2,1)}, bf16[32,384]{1,0:T(8,128)(2,1)}, f32[32,6]{1,0:T(8,128)}, f32[32,6]{1,0:T(8,128)}, bf16[4,32,384]{2,1,0:T(8,128)...) custom-call(bf16[32,384]{1,0:T(8,128)(2,1)} %x_ref.1, ...), custom_call_target="tpu_custom_call" | custom-call | tf_op jit(solution)/shard_map/moe_step/pallas_call | solution.py:267
  67.3 0.0 copy-start
  67.4 1.6 %copy-done = bf16[2,16,128,256]{3,2,1,0:T(8,128)(2,1)S(1)} copy-done((bf16[2,16,128,256]{3,2,1,0:T(8,128)(2,1)S(1)}, bf16[2,16,128,256]{3,2,1,0:T(8,128)(2,1)}, u32[]{:S(2)}) %copy-start) | copy-done | bytes 2097176
  68.9 0.0 copy-start.1
  68.9 1.6 %copy-done.1 = bf16[2,16,128,256]{3,2,1,0:T(8,128)(2,1)S(1)} copy-done((bf16[2,16,128,256]{3,2,1,0:T(8,128)(2,1)S(1)}, bf16[2,16,128,256]{3,2,1,0:T(8,128)(2,1)}, u32[]{:S(2)}) %copy-start.1) | copy-done | bytes 2097176
  70.5 0.0 copy-start.2
  70.5 1.6 %copy-done.2 = bf16[2,16,128,256]{3,2,1,0:T(8,128)(2,1)S(1)} copy-done((bf16[2,16,128,256]{3,2,1,0:T(8,128)(2,1)S(1)}, bf16[2,16,128,256]{3,2,1,0:T(8,128)(2,1)}, u32[]{:S(2)}) %copy-start.2) | copy-done | bytes 2097176
  72.1 0.0 copy-start.3
  72.1 0.9 copy-done.3
  73.0 0.0 copy-start.4
  73.0 0.9 copy-done.4
  73.9 0.0 copy-start.5
  73.9 0.9 copy-done.5
  74.8 0.0 copy-start.6
  74.8 0.9 copy-done.6
  75.7 0.0 copy-start.7
  75.7 0.9 copy-done.7
  76.6 0.0 copy-start.8
  76.6 0.9 copy-done.8
  77.5 0.0 copy-start.9
  77.5 0.7 copy-done.9
  78.2 0.0 copy-start.10
  78.2 0.7 copy-done.10
  79.0 0.0 copy-start.11
  79.0 0.7 copy-done.11
  79.7 0.0 copy-start.12
  79.7 0.7 copy-done.12
  80.4 15.1 %moe_grads.1 = (f32[16,384,256]{2,1,0:T(8,128)}, f32[16,384,256]{2,1,0:T(8,128)}, f32[16,256,384]{2,1,0:T(8,128)}, f32[16,384,256]{2,1,0:T(8,128)}, f32[16,384,2...) custom-call(bf16[128,384]{1,0:T(8,128)(2,1)S(1)} %bitcast.4, ...), custom_call_target="tpu_custom_call" | custom-call | tf_op jit(solution)/shard_map/moe_grads/pallas_call | solution.py:297
  95.6 0.7 copy.26
  96.2 0.7 copy.27
Async XLA Ops:
  67.3 1.6 %copy-start = (bf16[2,16,128,256]{3,2,1,0:T(8,128)(2,1)S(1)}, bf16[2,16,128,256]{3,2,1,0:T(8,128)(2,1)}, u32[]{:S(2)}) copy-start(bf16[2,16,128,256]{3,2,1,0:T(8,128)(2,1)} %get-tuple-element.39.h_ref) | copy-start | bytes 6291460
  68.9 1.6 %copy-start.1 = (bf16[2,16,128,256]{3,2,1,0:T(8,128)(2,1)S(1)}, bf16[2,16,128,256]{3,2,1,0:T(8,128)(2,1)}, u32[]{:S(2)}) copy-start(bf16[2,16,128,256]{3,2,1,0:T(8,128)(2,1)} %get-tuple-element.40.da_ref) | copy-start | bytes 6291460
  70.5 1.6 %copy-start.2 = (bf16[2,16,128,256]{3,2,1,0:T(8,128)(2,1)S(1)}, bf16[2,16,128,256]{3,2,1,0:T(8,128)(2,1)}, u32[]{:S(2)}) copy-start(bf16[2,16,128,256]{3,2,1,0:T(8,128)(2,1)} %get-tuple-element.41.db_ref) | copy-start | bytes 6291460
  72.1 0.9 copy-start.3
  73.0 0.9 copy-start.4
  73.9 0.9 copy-start.5
  74.8 0.9 copy-start.6
  75.7 0.9 copy-start.7
  76.6 0.9 copy-start.8
  77.5 0.7 copy-start.9
  78.2 0.7 copy-start.10
  79.0 0.7 copy-start.11
  79.7 0.7 copy-start.12

commit v2 on v1

v2 whole, which is shorter than its diff:
```python
import functools

import jax
import jax.numpy as jnp
from jax import lax
from jax.experimental import pallas as pl
from jax.experimental.pallas import tpu as pltpu
from jax.sharding import PartitionSpec as P

MESH = pl.DeviceIdType.MESH
F32 = jnp.float32
BF16 = jnp.bfloat16
NN = (((1,), (0,)), ((), ()))
NT = (((1,), (1,)), ((), ()))
TN = (((0,), (0,)), ((), ()))
LANES = 128
PAD = 8


def mm(lhs, rhs, dims=NN):
    return lax.dot_general(lhs, rhs, dims, preferred_element_type=F32)


def step_kernel(
    n, x_ref, dy_ref, idx_a_ref, idx_b_ref, gate_a_ref, gate_b_ref,
    w1_a, w3_a, w2_a, w1_b, w3_b, w2_b,
    x_out_ref, dx_in_ref, dgate_a_ref, dgate_b_ref, xa_out, xb_out, dya_out, dyb_out, ids_out, gates_out, h_out, da_out, db_out,
    w1_v, w3_v, w2_v, h_v, da_v, db_v, hf_v, dh_v, slope_v, silu_v,
    planes, meta, meta_own, square, ids_ref, gates_ref, xg_first, xg_a, xg_b, dyg_a, dyg_b,
    acc, acc_fwd, recv, own, dg, dg_send, dg_recv,
    w_sem, f_sem, o_sem, send_sem, recv_sem,
):
    local_experts = w1_a.shape[0]
    tok = x_ref.shape[0]
    top = idx_a_ref.shape[0]
    rows = n * tok
    me = lax.axis_index("ep")
    first_expert = me * local_experts
    weights = ((w1_a, w3_a, w2_a), (w1_b, w3_b, w2_b))
    slots = (w1_v, w3_v, w2_v)

    def weight_copy(layer, kind, e):
        return pltpu.make_async_copy(weights[layer][kind].at[e], slots[kind].at[layer, e], w_sem.at[layer, kind, e])

    for layer in range(2):
        for kind in range(3):
            @pl.loop(0, local_experts)
            def _(e):
                weight_copy(layer, kind, e).start()

    barrier = pltpu.get_barrier_semaphore()
    for k in range(1, n):
        pl.semaphore_signal(barrier, inc=1, device_id={"ep": lax.rem(me + k, n)}, device_id_type=MESH)
    pl.semaphore_wait(barrier, n - 1)

    def exchange(event, source, target):
        copies = []
        for k in (2, 1, 3):
            peer = lax.rem(me + k, n)
            copy = pltpu.make_async_remote_copy(
                src_ref=source(peer), dst_ref=target.at[me], send_sem=send_sem.at[event, k - 1], recv_sem=recv_sem.at[event, k - 1],
                device_id={"ep": peer}, device_id_type=MESH)
            copy.start()
            copies.append(copy)
        return copies

    def wait(copies):
        for copy in copies:
            copy.wait()

    first_x = exchange(0, lambda peer: x_ref, xg_first)
    xg_first[me] = x_ref[...]

    planes[...] = jnp.full_like(planes, -1.0)
    planes[0, 0:top, 0:tok] = idx_a_ref[...].astype(F32)
    planes[1, 0:top, 0:tok] = idx_b_ref[...].astype(F32)
    planes[2, 0:top, 0:tok] = gate_a_ref[...]
    planes[3, 0:top, 0:tok] = gate_b_ref[...]
    lane = lax.broadcasted_iota(jnp.int32, (PAD, LANES), 1)
    packed = planes[0]
    for p in range(1, 4):
        packed = jnp.where(lane < p * tok, packed, pltpu.roll(planes[p], p * tok, 1))
    meta_own[...] = packed
    meta[me] = packed
    sent_meta = exchange(1, lambda peer: meta_own, meta)
    sent_dy = exchange(2, lambda peer: dy_ref, dyg_b)
    dyg_b[me] = dy_ref[...]

    def read_meta():
        square[...] = jnp.full_like(square, -1.0)
        for kind in range(4):
            value = None
            for s in range(n):
                turned = pltpu.roll(meta[s], (s - kind) % n * tok, 1)
                value = turned if value is None else jnp.where(lane < s * tok, value, turned)
            square[kind * PAD:(kind + 1) * PAD, :] = value
        all_meta = square[...].T
        wide_lane = lax.broadcasted_iota(jnp.int32, (rows, LANES), 1)
        for layer in range(2):
            ids = pltpu.roll(all_meta, LANES - PAD, 1) if layer else all_meta
            ids_ref[layer] = jnp.where(wide_lane < top, ids, -1.0)
            gates_ref[layer] = pltpu.roll(all_meta, LANES - (2 + layer) * PAD, 1)

    def flat(ref):
        value = ref[...]
        return value.reshape(value.shape[0] * value.shape[1], value.shape[2])

    def pair_gate(layer, e):
        hit = ids_ref[layer] == (first_expert + e).astype(F32)
        gate = jnp.sum(jnp.where(hit, gates_ref[layer], 0.0), axis=1, keepdims=True)
        return hit, gate

    def hidden_of(layer, e, u_rows):
        pre_gate = mm(u_rows, w1_v[layer, e])
        pre_up = mm(u_rows, w3_v[layer, e])
        sig = jax.nn.sigmoid(pre_gate)
        silu = pre_gate * sig
        return pre_gate, pre_up, sig, silu, silu * pre_up

    def add_rows(total, value):
        total[...] += value.reshape(total.shape)

    def forward_hidden(layer, u_ref, first):
        u_rows = flat(u_ref)

        @pl.loop(0, local_experts)
        def _(e):
            if first:
                weight_copy(layer, 0, e).wait()
                weight_copy(layer, 1, e).wait()
            hf_v[e] = hidden_of(layer, e, u_rows)[4].astype(BF16)

    def forward_out(layer, total, first):
        total[...] = jnp.zeros_like(total)

        @pl.loop(0, local_experts)
        def _(e):
            if first:
                weight_copy(layer, 2, e).wait()
            gate = pair_gate(layer, e)[1]
            out_rows = mm(hf_v[e], w2_v[layer, e]).astype(BF16).astype(F32)
            add_rows(total, jnp.where(gate > 0.0, gate * out_rows, 0.0))

    def factor_copies(layer, e):
        return [pltpu.make_async_copy(v.at[layer, e], o.at[layer, e], f_sem.at[layer, i, e])
                for i, (v, o) in enumerate(((h_v, h_out), (da_v, da_out), (db_v, db_out)))]

    def d_hidden_of(layer, e, dy_rows, gate):
        q = (gate * dy_rows.astype(F32)).astype(BF16)
        return mm(q, w2_v[layer, e], NT)

    def put_back(layer, e, d_gate, d_up, total):
        da_v[layer, e] = d_gate
        db_v[layer, e] = d_up
        du = mm(d_gate, w1_v[layer, e], NT) + mm(d_up, w3_v[layer, e], NT)
        add_rows(total, du.astype(BF16).astype(F32))

    def gate_grads(layer, dy_all_ref):
        dg[layer] = jnp.zeros_like(dg[layer])
        dy_rows = flat(dy_all_ref)

        @pl.loop(0, local_experts)
        def _(e):
            hit = pair_gate(layer, e)[0]
            out_rows = mm(h_v[layer, e], w2_v[layer, e]).astype(BF16).astype(F32)
            dgate_col = jnp.sum(dy_rows.astype(F32) * out_rows, axis=1, keepdims=True)
            dg[layer] += jnp.where(hit, dgate_col, 0.0)

    def reduced(event, base, total):
        value = base.astype(F32) + total[me]
        for k in range(1, n):
            value += recv[event, lax.rem(me + k, n)]
        return value.astype(BF16)

    kept = ((xg_a, xa_out), (xg_b, xb_out), (dyg_a, dya_out), (dyg_b, dyb_out), (ids_ref, ids_out), (gates_ref, gates_out))

    def keep(*which):
        for i in which:
            pltpu.make_async_copy(kept[i][0], kept[i][1], o_sem.at[i]).start()

    wait(first_x)
    forward_hidden(0, xg_first, True)
    wait(sent_meta)
    read_meta()
    forward_out(0, acc, True)
    sent = exchange(3, lambda peer: acc.at[peer], recv.at[0])

    keep(4, 5)
    wait(sent_dy)
    keep(3)
    dy_b = flat(dyg_b)

    @pl.loop(0, local_experts)
    def _(e):
        weight_copy(1, 0, e).wait()
        weight_copy(1, 1, e).wait()
        weight_copy(1, 2, e).wait()
        dh_v[e] = d_hidden_of(1, e, dy_b, pair_gate(1, e)[1])

    wait(sent)
    x_mid = reduced(0, x_ref[...], acc)
    own[0] = x_mid
    xg_b[me] = x_mid
    sent_mid = exchange(4, lambda peer: own.at[0], xg_b)
    wait(sent_mid)
    keep(1)
    again = exchange(5, lambda peer: x_ref, xg_a)
    xg_a[me] = x_ref[...]

    acc[...] = jnp.zeros_like(acc)
    u_b = flat(xg_b)

    @pl.loop(0, local_experts)
    def _(e):
        pre_gate, pre_up, sig, silu, hidden = hidden_of(1, e, u_b)
        live = pair_gate(1, e)[1] > 0.0
        d_hidden = dh_v[e]
        d_gate = jnp.where(live, d_hidden * pre_up * sig * (1.0 + pre_gate * (1.0 - sig)), 0.0).astype(BF16)
        d_up = jnp.where(live, d_hidden * silu, 0.0).astype(BF16)
        h_v[1, e] = jnp.where(live, hidden, 0.0).astype(BF16)
        put_back(1, e, d_gate, d_up, acc)
        for copy in factor_copies(1, e):
            copy.start()

    sent = exchange(6, lambda peer: acc.at[peer], recv.at[1])

    gate_grads(1, dyg_b)
    forward_hidden(1, xg_b, False)
    forward_out(1, acc_fwd, False)
    wait(sent)
    dx_mid = reduced(1, dy_ref[...], acc)
    own[1] = dx_mid
    dyg_a[me] = dx_mid
    sent_mid = exchange(7, lambda peer: own.at[1], dyg_a)
    sent_out = exchange(8, lambda peer: acc_fwd.at[peer], recv.at[2])

    wait(again)
    keep(0)
    u_a = flat(xg_a)

    @pl.loop(0, local_experts)
    def _(e):
        pre_gate, pre_up, sig, silu, hidden = hidden_of(0, e, u_a)
        live = pair_gate(0, e)[1] > 0.0
        slope_v[e] = jnp.where(live, pre_up * sig * (1.0 + pre_gate * (1.0 - sig)), 0.0)
        silu_v[e] = jnp.where(live, silu, 0.0)
        h_v[0, e] = jnp.where(live, hidden, 0.0).astype(BF16)

    wait(sent_mid)
    keep(2)
    acc[...] = jnp.zeros_like(acc)
    dy_a = flat(dyg_a)

    @pl.loop(0, local_experts)
    def _(e):
        d_hidden = d_hidden_of(0, e, dy_a, pair_gate(0, e)[1])
        put_back(0, e, (d_hidden * slope_v[e]).astype(BF16), (d_hidden * silu_v[e]).astype(BF16), acc)
        for copy in factor_copies(0, e):
            copy.start()

    sent = exchange(9, lambda peer: acc.at[peer], recv.at[3])
    gate_grads(0, dyg_a)
    both = jnp.where(lax.broadcasted_iota(jnp.int32, (rows, LANES), 1) < PAD, dg[0], pltpu.roll(dg[1], PAD, 1)).T
    dg_send[...] = both[0:2 * PAD]
    sent_dg = exchange(10, lambda peer: dg_send, dg_recv)
    wait(sent_out)
    x_out_ref[...] = reduced(2, own[0], acc_fwd)
    for layer in range(2):
        @pl.loop(0, local_experts)
        def _(e):
            for copy in factor_copies(layer, e):
                copy.wait()
    for i, (source, target) in enumerate(kept):
        pltpu.make_async_copy(source, target, o_sem.at[i]).wait()
    wait(sent)
    dx_in_ref[...] = reduced(3, own[1], acc)
    wait(sent_dg)
    value = dg_send[...]
    for k in range(1, n):
        value += dg_recv[lax.rem(me + k, n)]
    value = pltpu.roll(value, lax.rem((n - me) * tok, rows), 1)
    dgate_a_ref[...] = value[0:top, 0:tok]
    dgate_b_ref[...] = value[PAD:PAD + top, 0:tok]


def grads_kernel(
    xa, xb, dya, dyb, ids_ref, gates_ref, h_ref, da_ref, db_ref, x_out_in, dx_in_in, dga_in, dgb_in,
    dw1_a, dw3_a, dw2_a, dw1_b, dw3_b, dw2_b, x_out, dx_in, dga, dgb,
):
    e = pl.program_id(0)
    expert = lax.axis_index("ep") * pl.num_programs(0) + e

    @pl.when(e == 0)
    def _():
        x_out[...] = x_out_in[...]
        dx_in[...] = dx_in_in[...]
        dga[...] = dga_in[...]
        dgb[...] = dgb_in[...]

    for layer, (x, dy, dw1, dw3, dw2) in enumerate(((xa, dya, dw1_a, dw3_a, dw2_a), (xb, dyb, dw1_b, dw3_b, dw2_b))):
        gate = jnp.sum(jnp.where(ids_ref[layer] == expert.astype(F32), gates_ref[layer], 0.0), axis=1, keepdims=True)
        q = (gate * dy[...].astype(F32)).astype(BF16)
        dw2[0] = mm(h_ref[layer, 0], q, TN)
        dw1[0] = mm(x[...], da_ref[layer, 0], TN)
        dw3[0] = mm(x[...], db_ref[layer, 0], TN)


def solution(mesh):
    n = mesh.shape["ep"]
    tok_spec = P(("dp", "ep"))
    w_spec = P("ep")

    def device_program(x_in, idx_a, idx_b, gate_a, gate_b, dy_out, w1_a, w3_a, w2_a, w1_b, w3_b, w2_b):
        tok, width = x_in.shape
        top = idx_a.shape[1]
        experts, _, ff = w1_a.shape
        rows = n * tok
        vmem = pl.BlockSpec(memory_space=pltpu.VMEM)
        anyw = pl.BlockSpec(memory_space=pl.ANY)
        sds = jax.ShapeDtypeStruct
        factor = sds((2, experts, rows, ff), BF16)
        gathered = sds((n, tok, width), BF16)
        tokens = pltpu.VMEM((n, tok, width), BF16)
        sums = pltpu.VMEM((n, tok, width), F32)
        outs = pl.pallas_call(
            functools.partial(step_kernel, n),
            out_shape=(
                sds((tok, width), BF16), sds((tok, width), BF16), sds((top, tok), F32), sds((top, tok), F32),
                gathered, gathered, gathered, gathered,
                sds((2, rows, LANES), F32), sds((2, rows, LANES), F32), factor, factor, factor),
            in_specs=[vmem] * 6 + [anyw] * 6,
            out_specs=(vmem,) * 4 + (anyw,) * 9,
            scratch_shapes=[
                pltpu.VMEM((2, experts, width, ff), BF16), pltpu.VMEM((2, experts, width, ff), BF16), pltpu.VMEM((2, experts, ff, width), BF16),
                pltpu.VMEM((2, experts, rows, ff), BF16), pltpu.VMEM((2, experts, rows, ff), BF16), pltpu.VMEM((2, experts, rows, ff), BF16),
                pltpu.VMEM((experts, rows, ff), BF16), pltpu.VMEM((experts, rows, ff), F32), pltpu.VMEM((experts, rows, ff), F32), pltpu.VMEM((experts, rows, ff), F32),
                pltpu.VMEM((4, PAD, LANES), F32), pltpu.VMEM((n, PAD, LANES), F32), pltpu.VMEM((PAD, LANES), F32), pltpu.VMEM((LANES, LANES), F32),
                pltpu.VMEM((2, rows, LANES), F32), pltpu.VMEM((2, rows, LANES), F32),
                tokens, tokens, tokens, tokens, tokens,
                sums, sums, pltpu.VMEM((4, n, tok, width), F32), pltpu.VMEM((2, tok, width), BF16),
                pltpu.VMEM((2, rows, LANES), F32), pltpu.VMEM((2 * PAD, LANES), F32), pltpu.VMEM((n, 2 * PAD, LANES), F32),
                pltpu.SemaphoreType.DMA((2, 3, experts)), pltpu.SemaphoreType.DMA((2, 3, experts)), pltpu.SemaphoreType.DMA((6,)),
                pltpu.SemaphoreType.DMA((11, n - 1)), pltpu.SemaphoreType.DMA((11, n - 1)),
            ],
            compiler_params=pltpu.CompilerParams(collective_id=0, has_side_effects=True, vmem_limit_bytes=56 << 20),
            name="moe_step",
        )(x_in, dy_out, idx_a.T, idx_b.T, gate_a.T, gate_b.T, w1_a, w3_a, w2_a, w1_b, w3_b, w2_b)
        x_out, dx_in, dga, dgb, xa, xb, dya, dyb, ids, gates, h, da, db = outs
        flat = lambda v: v.reshape(rows, width)
        whole = lambda v: pl.BlockSpec(v.shape, lambda e: (0,) * v.ndim)
        fac = pl.BlockSpec((2, 1, rows, ff), lambda e: (0, e, 0, 0))
        dw_up = pl.BlockSpec((1, width, ff), lambda e: (e, 0, 0))
        dw_down = pl.BlockSpec((1, ff, width), lambda e: (e, 0, 0))
        small = [flat(xa), flat(xb), flat(dya), flat(dyb), ids, gates]
        last = [x_out, dx_in, dga, dgb]
        up, down = sds((experts, width, ff), F32), sds((experts, ff, width), F32)
        res = pl.pallas_call(
            grads_kernel,
            grid=(experts,),
            out_shape=(up, up, down, up, up, down) + tuple(sds(v.shape, v.dtype) for v in last),
            in_specs=[whole(v) for v in small] + [fac] * 3 + [whole(v) for v in last],
            out_specs=(dw_up, dw_up, dw_down, dw_up, dw_up, dw_down) + tuple(whole(v) for v in last),
            compiler_params=pltpu.CompilerParams(dimension_semantics=("arbitrary",), vmem_limit_bytes=63 << 20),
            name="moe_grads",
        )(*small, h, da, db, *last)
        g = res[:6]
        x_out, dx_in, dga, dgb = res[6:]
        return (x_out, dx_in) + g + (dga.T, dgb.T)

    return jax.shard_map(device_program, mesh=mesh, in_specs=(tok_spec,) * 6 + (w_spec,) * 6, out_specs=(tok_spec,) * 10, check_vma=False)
```

time: 97.7 us -> 83.7 us (0.86)
  local copies, waits for them, and re-layouts: 19.9 us -> 0 us
  Pallas kernels: 76.4 us -> 82.4 us
    unnamed x32 -> x0, local copies, waits for them, and re-layouts: 19.9 us -> none
    pallas_call x1, Pallas kernels: 15.1 us -> 18.9 us  [device_program(): pl.pallas_call(grads_kernel, grid=(experts,), out_shape=(up, up, down, up...]
    pallas_call x1, Pallas kernels: 61.2 us -> 63.5 us  [device_program(): pl.pallas_call(functools.partial(step_kernel, n), out_shape=(sds((tok, wi...]
where the time goes in v2:
time: 83.7 us; the launch traced here: 83.1 us
  Pallas kernels  82.4 us (98%)
    pallas_call x1, Pallas kernels, device_program(): pl.pallas_call(functools.partial(step_kernel, n), out_shape=(sds((tok, wi...  63.5 us
    pallas_call x1, Pallas kernels, device_program(): pl.pallas_call(grads_kernel, grid=(experts,), out_shape=(up, up, down, up...  18.9 us

profile of v2, /device:TPU:0, one launch (start us, length us, event | category | flops | bytes accessed | tf_op | source)
XLA Modules:
  0.0 83.1 jit_solution(1843078435823292771)
XLA Ops:
  0.6 63.5 %moe_step.1 = (bf16[32,384]{1,0:T(8,128)(2,1)}, bf16[32,384]{1,0:T(8,128)(2,1)}, f32[6,32]{1,0:T(8,128)}, f32[6,32]{1,0:T(8,128)}, bf16[4,32,384]{2,1,0:T(8,128)...) custom-call(bf16[32,384]{1,0:T(8,128)(2,1)} %x_ref.1, ...), custom_call_target="tpu_custom_call" | custom-call | tf_op jit(solution)/shard_map/moe_step/pallas_call | solution.py:325
  64.2 18.9 %moe_grads.1 = (f32[16,384,256]{2,1,0:T(8,128)}, f32[16,384,256]{2,1,0:T(8,128)}, f32[16,256,384]{2,1,0:T(8,128)}, f32[16,384,256]{2,1,0:T(8,128)}, f32[16,384,2...) custom-call(bf16[128,384]{1,0:T(8,128)(2,1)} %bitcast.10, ...), custom_call_target="tpu_custom_call" | custom-call | tf_op jit(solution)/shard_map/moe_grads/pallas_call | solution.py:357
